TPU v7x, 32 devices: a whole 2x2x4 slice. The times are simulated.
32 devices in a mesh: section: 8 (over z, y), fsdp: 4 (over x, core).
Axes of the slice: x: 2, y: 2, z: 4, core: 2. Of those that a mesh axis runs over, the one named last changes fastest.
Arguments:
- source_rows: bfloat16 [3072, 4096], P(('section', 'fsdp')), may hold values from -6 to 6
- target_rows: bfloat16 [1024, 4096], P('section'), may hold values from -6 to 6
- attn_weights: bfloat16 [8, 4, 4096, 3072], P('section', None, None, 'fsdp'), may hold values from -3.76875 to 3.76875
- gains: float32 [8, 4096], P('section'), may hold values from 0.25 to 1.75
- lengths: int32 [8], P('section'), may hold values from 192 to 384
Outputs:
- source_next: bfloat16 [3072, 4096], P(('section', 'fsdp'))
- target_next: bfloat16 [1024, 4096], P('section')
Inputs may be any that keep to these rules, and one draw needn't show every extreme that they name: Keys at positions lengths[s] and beyond are padding.
All inputs are finite; a program needn't handle non-finite values.
Results may differ from a plain program's by a relative error of at most 0.015.
The roundings to bfloat16 on the way count: a program that leaves them out, or rounds other values in their place, can miss the bound.
Values may be sent and summed in bfloat16 or wider, within the bound.
A program may use at most 128 MiB of HBM per device.

v0:
```python
import jax
import jax.numpy as jnp
from jax import lax
from jax.sharding import PartitionSpec as P

HEAD_DIM = 64


def shifted(value, axis, steps):
    count = lax.axis_size(axis)
    pairs = [(source, (source + steps) % count) for source in range(count)]
    return lax.ppermute(value, axis, pairs)


def rms_norm(block_rows, gain_row):
    widened = block_rows.astype(jnp.float32)
    inverse_rms = lax.rsqrt(jnp.mean(widened * widened, axis=-1, keepdims=True) + 1e-06)
    return (widened * inverse_rms * gain_row).astype(jnp.bfloat16)


def project(block_rows, weight):
    return jnp.dot(block_rows, weight, preferred_element_type=jnp.float32).astype(jnp.bfloat16)


def attend(queries, key_rows, values, length):
    query_count = queries.shape[0]
    key_count = key_rows.shape[0]
    head_count = queries.shape[1] // HEAD_DIM
    query_heads = queries.reshape(query_count, head_count, HEAD_DIM)
    key_heads = key_rows.reshape(key_count, head_count, HEAD_DIM)
    value_heads = values.reshape(key_count, head_count, HEAD_DIM)
    scores = (
        jnp.einsum("qhc,khc->hqk", query_heads, key_heads, preferred_element_type=jnp.float32)
        * 0.125
    )
    key_valid = jnp.arange(key_count, dtype=jnp.int32) < length
    scores = jnp.where(key_valid[None, None, :], scores, -1000000000.0)
    row_max = jnp.max(scores, axis=-1, keepdims=True)
    expo = jnp.exp(scores - row_max)
    soft = (expo / jnp.sum(expo, axis=-1, keepdims=True)).astype(jnp.bfloat16)
    context = jnp.einsum("hqk,khc->qhc", soft, value_heads, preferred_element_type=jnp.float32)
    return context.reshape(query_count, head_count * HEAD_DIM).astype(jnp.bfloat16)


def out_partial(context, out_weight):
    return lax.dot_general(
        context, out_weight, (((1,), (1,)), ((), ())), preferred_element_type=jnp.float32
    )


def local(source_rows, target_rows, attn_weights, gains, lengths):
    section_index = lax.axis_index("section")
    encoder_section = section_index < lax.axis_size("section") // 2
    weights = attn_weights[0]
    gain_row = gains[0]
    length = lengths[0]
    source_whole = lax.all_gather(source_rows, "fsdp", axis=0, tiled=True)

    def encoder_work(whole_rows, target_block):
        normed = rms_norm(whole_rows, gain_row)
        context = attend(
            project(normed, weights[0]),
            project(normed, weights[1]),
            project(normed, weights[2]),
            length,
        )
        return (out_partial(context, weights[3]), jnp.zeros(target_block.shape, jnp.float32))

    def decoder_work(whole_rows, target_block):
        normed = rms_norm(target_block, gain_row)
        context = attend(
            project(normed, weights[0]),
            project(whole_rows, weights[1]),
            project(whole_rows, weights[2]),
            length,
        )
        return (jnp.zeros(whole_rows.shape, jnp.float32), out_partial(context, weights[3]))

    source_terms, target_terms = lax.cond(
        encoder_section, encoder_work, decoder_work, source_whole, target_rows
    )
    source_sum = lax.psum_scatter(
        source_terms.astype(jnp.bfloat16), "fsdp", scatter_dimension=0, tiled=True
    ).astype(jnp.float32)
    source_new = (source_rows.astype(jnp.float32) + source_sum).astype(jnp.bfloat16)
    target_sum = lax.psum(target_terms.astype(jnp.bfloat16), "fsdp").astype(jnp.float32)
    target_new = (target_rows.astype(jnp.float32) + target_sum).astype(jnp.bfloat16)
    source_next, target_next = shifted((source_new, target_new), "section", 1)
    return (source_next, target_next)


def solution(mesh):
    in_specs = (
        P(("section", "fsdp"), None),
        P("section", None),
        P("section", None, None, "fsdp"),
        P("section", None),
        P("section"),
    )
    out_specs = (P(("section", "fsdp"), None), P("section", None))
    return jax.shard_map(local, mesh=mesh, in_specs=in_specs, out_specs=out_specs, check_vma=False)
```

profile of v0, /device:TPU:0, one launch (start us, length us, event | category | flops | bytes accessed | tf_op | source)
XLA Modules:
  0.0 194.1 jit_solution(7510881435808563548)
XLA Ops:
  7.2 0.7 all-gather.2.cloned.1.call-update
  7.9 32.8 %all-gather.2.cloned.1.call-done = bf16[384,4096]{1,0:T(8,128)(2,1)} async-done(((bf16[96,4096]{1,0:T(8,128)(2,1)}), bf16[384,4096]{1,0:T(8,128)(2,1)}) %all-gather.2.cloned.1.call-update) | async-done | bytes 3145744 | tf_op jit(solution)/shard_map/all_gather | solution.py:57
  40.8 46.0 %conditional.1 = (bf16[384,4096]{1,0:T(8,128)(2,1)S(1)}, bf16[128,4096]{1,0:T(8,128)(2,1)}) conditional(s32[]{:T(128)} %convert_element_type.82, (bf16[4,4096,768]{2,1,0:T(8,128)(2,1)}, bf16[384,4096]{1,0:T(8,128)(2,1)}, s32[]{:T(128)}, bf16[128,4096]{1,0:T(8,128)(2,1)}, f32[1,4096]{1,0:T(1,128)}) %tuple.31, (bf16[384,4096]{1,0:T(8,128)(2,1)}, ...), branch_computations={%region_0.4_spmd, %region_4.8_spmd} | conditional | flops 10152052736 | bytes 77100880 | solution.py:79
  40.8 2.6 %fusion.39 = f32[384]{0:T(512)S(1)} fusion(bf16[384,4096]{1,0:T(8,128)(2,1)} %get-tuple-element.23), kind=kLoop, calls=%fused_computation.43 | loop fusion | flops 4718208 | bytes 3147264 | tf_op jit(solution)/shard_map/cond/branch_1_fun/reduce_sum | solution.py:17
  43.4 7.4 %fusion.63 = bf16[384,768]{1,0:T(8,128)(2,1)} fusion(bf16[4,4096,768]{2,1,0:T(8,128)(2,1)} %get-tuple-element.25, bf16[384,4096]{1,0:T(8,128)(2,1)} %get-tuple-element.23, f32[4096]{0:T(1024)} %bitcast.73, f32[384]{0:T(512)S(1)} %add_rsqrt_fusion.1), kind=kOutput, calls=%fused_computation.65 | convolution fusion | flops 2422505472 | bytes 10044928 | tf_op jit(solution)/shard_map/cond/branch_1_fun/dot_general | solution.py:22
  50.8 2.1 %copy.18 = bf16[384,768]{0,1:T(8,128)(2,1)} copy(bf16[384,768]{1,0:T(8,128)(2,1)} %fusion.63) | data formatting | bytes 1179648 | tf_op jit(solution)/shard_map/cond/branch_1_fun/convert_element_type | solution.py:22
  52.9 6.3 %fusion.66 = bf16[384,768]{1,0:T(8,128)(2,1)} fusion(bf16[4,4096,768]{2,1,0:T(8,128)(2,1)} %get-tuple-element.25, bf16[384,4096]{1,0:T(8,128)(2,1)S(1)} %copy-done.2, f32[4096]{0:T(1024)S(1)} %bitcast.74, f32[384]{0:T(512)S(1)} %add_rsqrt_fusion.1), kind=kOutput, calls=%fused_computation.66 | convolution fusion | flops 2422505472 | bytes 10044928 | tf_op jit(solution)/shard_map/cond/branch_1_fun/dot_general | solution.py:22
  59.2 2.1 %copy.19 = bf16[384,768]{0,1:T(8,128)(2,1)} copy(bf16[384,768]{1,0:T(8,128)(2,1)} %fusion.66) | data formatting | bytes 1179648 | tf_op jit(solution)/shard_map/cond/branch_1_fun/convert_element_type | solution.py:22
  62.0 7.0 %fusion.77 = (f32[12,384]{1,0:T(8,128)S(1)}, f32[12,384,384]{1,2,0:T(8,128)}) fusion(pred[384]{0:T(512)(128)(4,1)S(1)} %iota_compare_fusion.1, bf16[384,12,64]{0,2,1:T(8,128)(2,1)} %bitcast.64, bf16[384,12,64]{0,2,1:T(8,128)(2,1)} %bitcast.66), kind=kOutput, calls=%fused_computation.75 | convolution fusion | flops 233570688 | bytes 8276352 | tf_op jit(solution)/shard_map/cond/branch_1_fun/sub | solution.py:39
  68.9 6.3 %fusion.60 = bf16[384,768]{1,0:T(8,128)(2,1)} fusion(bf16[4,4096,768]{2,1,0:T(8,128)(2,1)} %get-tuple-element.25, bf16[384,4096]{1,0:T(8,128)(2,1)S(1)} %copy-done.2, f32[4096]{0:T(1024)S(1)} %bitcast.75, f32[384]{0:T(512)S(1)} %add_rsqrt_fusion.1), kind=kOutput, calls=%fused_computation.64 | convolution fusion | flops 2422505472 | bytes 10044928 | tf_op jit(solution)/shard_map/cond/branch_1_fun/dot_general | solution.py:22
  75.2 1.4 copy.17
  76.5 3.7 %fusion.59 = bf16[12,64,384]{2,1,0:T(8,128)(2,1)S(1)} fusion(bf16[384,12,64]{0,2,1:T(8,128)(2,1)S(1)} %bitcast.68, f32[12,384,384]{1,2,0:T(8,128)} %get-tuple-element.36, f32[12,384]{1,0:T(8,128)S(1)} %get-tuple-element.35), kind=kOutput, calls=%fused_computation.63 | convolution fusion | flops 230326272 | bytes 8275968 | tf_op jit(solution)/shard_map/cond/branch_1_fun/hqk,khc->qhc/dot_general | solution.py:41
  80.3 5.4 %fusion.42 = bf16[384,4096]{1,0:T(8,128)(2,1)S(1)} fusion(bf16[384,768]{0,1:T(8,128)(2,1)S(1)} %bitcast.76, bf16[4,4096,768]{2,1,0:T(8,128)(2,1)} %get-tuple-element.25), kind=kOutput, calls=%fused_computation.46 | convolution fusion | flops 2415919104 | bytes 10027008 | tf_op jit(solution)/shard_map/cond/branch_1_fun/dot_general | solution.py:46
  85.7 1.1 broadcast.57
  86.9 1.6 copy-done
  88.5 32.9 %all-reduce.2.cloned.1.call-done = bf16[128,4096]{1,0:T(8,128)(2,1)} async-done(((bf16[128,4096]{1,0:T(8,128)(2,1)}), bf16[128,4096]{1,0:T(8,128)(2,1)}) %all-reduce.2.cloned.1.call-update) | async-done | bytes 1048592 | tf_op jit(solution)/shard_map/psum | solution.py:86
  121.4 1.8 add_convert_fusion
  123.2 1.5 collective-permute-start.1
  124.7 37.6 %reduce-scatter.2.cloned.1.call-done = bf16[96,4096]{1,0:T(8,128)(2,1)} async-done(((bf16[384,4096]{1,0:T(8,128)(2,1)}), bf16[96,4096]{1,0:T(8,128)(2,1)}) %reduce-scatter.2.cloned.1.call-update) | async-done | bytes 786448 | tf_op jit(solution)/shard_map/reduce_scatter | solution.py:82
  162.3 1.6 add_convert_fusion.1
  163.9 1.5 collective-permute-start
  165.4 20.3 %collective-permute-done = bf16[96,4096]{1,0:T(8,128)(2,1)S(1)} collective-permute-done((bf16[96,4096]{1,0:T(8,128)(2,1)S(1)}, bf16[96,4096]{1,0:T(8,128)(2,1)S(1)}, u32[]{:S(2)}, u32[]{:S(2)}) %collective-permute-start) | collective-permute-done | bytes 786464 | tf_op jit(solution)/shard_map/ppermute | solution.py:12
  185.8 0.9 copy.29
  186.6 1.0 copy.30
  (13 shorter events, 0.8 us)
Async XLA Ops:
  7.2 33.6 %all-gather.2.cloned.1.call-start = ((), (), s32[]{:S(2)}) async-start(), calls=%async_computation.1 | async-start | bytes 3932160 | tf_op jit(solution)/shard_map/all_gather | solution.py:57
  7.9 113.5 %all-reduce.2.cloned.1.call-start = ((), (), s32[]{:S(2)}) async-start(), calls=%async_computation.3 | async-start | bytes 2097152 | tf_op jit(solution)/shard_map/psum | solution.py:86
  43.4 9.5 %copy-start.2 = (bf16[384,4096]{1,0:T(8,128)(2,1)S(1)}, bf16[384,4096]{1,0:T(8,128)(2,1)}, u32[]{:S(2)}) copy-start(bf16[384,4096]{1,0:T(8,128)(2,1)} %get-tuple-element.23) | copy-start | bytes 9437188 | tf_op jit(solution)/shard_map/cond
  43.4 9.5 %copy-start.3 = (f32[1,4096]{1,0:T(1,128)S(1)}, f32[1,4096]{1,0:T(1,128)}, u32[]{:S(2)}) copy-start(f32[1,4096]{1,0:T(1,128)} %get-tuple-element.24) | copy-start | bytes 49156 | tf_op jit(solution)/shard_map/cond
  86.8 1.7 copy-start
  86.8 75.5 %reduce-scatter.2.cloned.1.call-start = ((), (), s32[]{:S(2)}) async-start(), calls=%async_computation.2 | async-start | bytes 3932160 | tf_op jit(solution)/shard_map/reduce_scatter | solution.py:82
  123.2 42.2 %collective-permute-start.1 = (bf16[128,4096]{1,0:T(8,128)(2,1)S(1)}, bf16[128,4096]{1,0:T(8,128)(2,1)S(1)}, u32[]{:S(2)}, u32[]{:S(2)}) collective-permute-start(bf16[128,4096]{1,0:T(8,128)(2,1)S(1)} %add_convert_fusion), channel_id=1, source_target_pairs={{0,4},{4,8},{8,12},{12,16},{16,20},{20,24},{24,28},{28,0},{1,5},{5... | collective-permute-start | bytes 3145736 | tf_op jit(solution)/shard_map/ppermute | solution.py:12
  163.9 21.9 %collective-permute-start = (bf16[96,4096]{1,0:T(8,128)(2,1)S(1)}, bf16[96,4096]{1,0:T(8,128)(2,1)S(1)}, u32[]{:S(2)}, u32[]{:S(2)}) collective-permute-start(bf16[96,4096]{1,0:T(8,128)(2,1)S(1)} %add_convert_fusion.1), channel_id=1, source_target_pairs={{0,4},{4,8},{8,12},{12,16},{16,20},{20,24},{24,28},{28,0},{1,5},{5... | collective-permute-start | bytes 2359304 | tf_op jit(solution)/shard_map/ppermute | solution.py:12
Sparse Core Ops, SparseCore 0:
  9.5 31.2 all-gather.1
  86.9 34.4 all-reduce.1
  123.9 38.3 reduce-scatter.1
where the time goes:
time: 195 us; the launch traced here: 194 us
  waiting for transfers between devices  124 us (64%)
  matrix products  36 us (18%)
  between operations  13.8 us (7%)
  local copies, waits for them, and re-layouts  10.1 us (5%)
  other arithmetic  6.59 us (3%)
  starting transfers between devices  3.17 us (2%)
    reduce_scatter x1, waiting for transfers between devices, local(): lax.psum_scatter(source_terms.astype(jnp.bfloat16), 'fsdp', scatter_dimen...  37.6 us
    psum x1, waiting for transfers between devices, local(): lax.psum(target_terms.astype(jnp.bfloat16), 'fsdp').astype(jnp.float32)  32.9 us
    all_gather x1, waiting for transfers between devices, local(): source_whole = lax.all_gather(source_rows, 'fsdp', axis=0, tiled=True)  32.8 us
    ppermute x2, waiting for transfers between devices, shifted(): return lax.ppermute(value, axis, pairs)  20.3 us
    dot_general x3, matrix products, project(): jnp.dot(block_rows, weight, preferred_element_type=jnp.float32)  19.9 us
    sub x1, matrix products, attend(): expo = jnp.exp(scores - row_max)  6.96 us
    convert_element_type x3, local copies, waits for them, and re-layouts, project(): jnp.dot(block_rows, weight, preferred_element_type=jnp.float32)  5.62 us
    dot_general x1, matrix products, out_partial(): lax.dot_general(context, out_weight, (((1,), (1,)), ((), ())), preferred_...  5.45 us
  transfers between devices with their start and end apart: 5, of which 4 were waited for; matrix products, arithmetic and copies ran while one was open for 2% of the time, Pallas kernels for 0%

commit v1 on v0

--- a/solution.py
+++ b/solution.py
@@ -54,7 +54,12 @@
     weights = attn_weights[0]
     gain_row = gains[0]
     length = lengths[0]
-    source_whole = lax.all_gather(source_rows, "fsdp", axis=0, tiled=True)
+    ring = [source_rows]
+    for hop in range(3):
+        ring.append(lax.ppermute(ring[-1], "fsdp", [(dev, (dev + 1) % 4) for dev in range(4)]))
+    source_whole = jnp.roll(
+        jnp.concatenate(ring[::-1], axis=0), (lax.axis_index("fsdp") + 1) * ring[0].shape[0], axis=0
+    )
 
     def encoder_work(whole_rows, target_block):
         normed = rms_norm(whole_rows, gain_row)

time: 195 us -> 199 us (1.021)
  waiting for transfers between devices: 124 us -> 129 us
  other arithmetic: 6.59 us -> 4.46 us
    ppermute x0 -> x3, waiting for transfers between devices: none -> 34.6 us  [local(): lax.ppermute(ring[-1], 'fsdp', [(dev, (dev + 1) % 4) for dev in range(4)])]
    all_gather x1 -> x0, waiting for transfers between devices: 32.8 us -> none  [local(): source_whole = lax.all_gather(source_rows, 'fsdp', axis=0, tiled=True)]
    psum x1, waiting for transfers between devices: 32.9 us -> 35.7 us  [local(): lax.psum(target_terms.astype(jnp.bfloat16), 'fsdp').astype(jnp.float32)]
  transfers between devices with their start and end apart: 5 -> 7, of which waited for: 4 -> 6; matrix products, arithmetic and copies ran while one was open for 2% -> 2% of each run, Pallas kernels for 0% -> 0%
where the time goes in v1:
time: 199 us; the launch traced here: 198 us
  waiting for transfers between devices  129 us (65%)
  matrix products  36.3 us (18%)
  between operations  14.2 us (7%)
  local copies, waits for them, and re-layouts  10.3 us (5%)
  other arithmetic  4.46 us (2%)
  starting transfers between devices  3.72 us (2%)
    reduce_scatter x1, waiting for transfers between devices, local(): lax.psum_scatter(source_terms.astype(jnp.bfloat16), 'fsdp', scatter_dimen...  37.6 us
    psum x1, waiting for transfers between devices, local(): lax.psum(target_terms.astype(jnp.bfloat16), 'fsdp').astype(jnp.float32)  35.7 us
    ppermute x3, waiting for transfers between devices, local(): lax.ppermute(ring[-1], 'fsdp', [(dev, (dev + 1) % 4) for dev in range(4)])  34.6 us
    ppermute x2, waiting for transfers between devices, shifted(): return lax.ppermute(value, axis, pairs)  20.3 us
    dot_general x3, matrix products, project(): jnp.dot(block_rows, weight, preferred_element_type=jnp.float32)  18.8 us
    dot_general x1, matrix products, out_partial(): lax.dot_general(context, out_weight, (((1,), (1,)), ((), ())), preferred_...  7.12 us
    sub x1, matrix products, attend(): expo = jnp.exp(scores - row_max)  6.78 us
    convert_element_type x3, local copies, waits for them, and re-layouts, project(): jnp.dot(block_rows, weight, preferred_element_type=jnp.float32)  4.85 us
  transfers between devices with their start and end apart: 7, of which 6 were waited for; matrix products, arithmetic and copies ran while one was open for 2% of the time, Pallas kernels for 0%

profile of v1, /device:TPU:0, one launch (start us, length us, event | category | flops | bytes accessed | tf_op | source)
XLA Modules:
  0.0 198.0 jit_solution(8622282099075192465)
XLA Ops:
  7.8 11.8 %collective-permute-done = bf16[96,4096]{1,0:T(8,128)(2,1)S(1)} collective-permute-done((bf16[96,4096]{1,0:T(8,128)(2,1)}, bf16[96,4096]{1,0:T(8,128)(2,1)S(1)}, u32[]{:S(2)}, u32[]{:S(2)}) %collective-permute-start) | collective-permute-done | bytes 786464 | tf_op jit(solution)/shard_map/ppermute | solution.py:59
  19.6 11.4 %collective-permute-done.1 = bf16[96,4096]{1,0:T(8,128)(2,1)S(1)} collective-permute-done((bf16[96,4096]{1,0:T(8,128)(2,1)S(1)}, bf16[96,4096]{1,0:T(8,128)(2,1)S(1)}, u32[]{:S(2)}, u32[]{:S(2)}) %collective-permute-start.1) | collective-permute-done | bytes 786464 | tf_op jit(solution)/shard_map/ppermute | solution.py:59
  31.0 11.4 %collective-permute-done.2 = bf16[96,4096]{1,0:T(8,128)(2,1)S(1)} collective-permute-done((bf16[96,4096]{1,0:T(8,128)(2,1)S(1)}, bf16[96,4096]{1,0:T(8,128)(2,1)S(1)}, u32[]{:S(2)}, u32[]{:S(2)}) %collective-permute-start.2) | collective-permute-done | bytes 786464 | tf_op jit(solution)/shard_map/ppermute | solution.py:59
  42.6 1.2 constant_dynamic-update-slice_fusion.4
  45.0 43.7 %conditional.1 = (bf16[384,4096]{1,0:T(8,128)(2,1)}, bf16[128,4096]{1,0:T(8,128)(2,1)}) conditional(s32[]{:T(128)} %convert_element_type.82, (bf16[4,4096,768]{2,1,0:T(8,128)(2,1)}, bf16[384,4096]{1,0:T(8,128)(2,1)S(1)}, s32[]{:T(128)}, bf16[128,4096]{1,0:T(8,128)(2,1)S(1)}, f32[1,4096]{1,0:T(1,128)S(1)}) %tuple.32, (bf16[384,4096]{1,0:T(8,128)(2,1)S(1)}, ...), branch_computations={%region_0.4_spmd, %region_4.8_spmd} | conditional | flops 10152052736 | bytes 64452376 | solution.py:84
  46.4 6.3 %fusion.63 = bf16[384,768]{1,0:T(8,128)(2,1)} fusion(bf16[4,4096,768]{2,1,0:T(8,128)(2,1)} %get-tuple-element.25, bf16[384,4096]{1,0:T(8,128)(2,1)S(1)} %get-tuple-element.23, f32[4096]{0:T(1024)S(1)} %bitcast.73, f32[384]{0:T(512)S(1)} %add_rsqrt_fusion.1), kind=kOutput, calls=%fused_computation.65 | convolution fusion | flops 2422505472 | bytes 10044928 | tf_op jit(solution)/shard_map/cond/branch_1_fun/dot_general | solution.py:22
  52.7 2.1 %copy.18 = bf16[384,768]{0,1:T(8,128)(2,1)} copy(bf16[384,768]{1,0:T(8,128)(2,1)} %fusion.63) | data formatting | bytes 1179648 | tf_op jit(solution)/shard_map/cond/branch_1_fun/convert_element_type | solution.py:22
  54.8 6.3 %fusion.66 = bf16[384,768]{1,0:T(8,128)(2,1)} fusion(bf16[4,4096,768]{2,1,0:T(8,128)(2,1)} %get-tuple-element.25, bf16[384,4096]{1,0:T(8,128)(2,1)S(1)} %get-tuple-element.23, f32[4096]{0:T(1024)S(1)} %bitcast.74, f32[384]{0:T(512)S(1)} %add_rsqrt_fusion.1), kind=kOutput, calls=%fused_computation.66 | convolution fusion | flops 2422505472 | bytes 10044928 | tf_op jit(solution)/shard_map/cond/branch_1_fun/dot_general | solution.py:22
  61.0 6.3 %fusion.60 = bf16[384,768]{1,0:T(8,128)(2,1)} fusion(bf16[4,4096,768]{2,1,0:T(8,128)(2,1)} %get-tuple-element.25, bf16[384,4096]{1,0:T(8,128)(2,1)S(1)} %get-tuple-element.23, f32[4096]{0:T(1024)S(1)} %bitcast.75, f32[384]{0:T(512)S(1)} %add_rsqrt_fusion.1), kind=kOutput, calls=%fused_computation.64 | convolution fusion | flops 2422505472 | bytes 10044928 | tf_op jit(solution)/shard_map/cond/branch_1_fun/dot_general | solution.py:22
  67.3 1.4 copy.17
  68.6 1.4 copy.19
  70.0 6.8 %fusion.77 = (f32[12,384]{1,0:T(8,128)S(1)}, f32[12,384,384]{1,2,0:T(8,128)}) fusion(pred[384]{0:T(512)(128)(4,1)S(1)} %iota_compare_fusion.1, bf16[384,12,64]{0,2,1:T(8,128)(2,1)} %bitcast.64, bf16[384,12,64]{0,2,1:T(8,128)(2,1)S(1)} %bitcast.68), kind=kOutput, calls=%fused_computation.84 | convolution fusion | flops 233570688 | bytes 8276352 | tf_op jit(solution)/shard_map/cond/branch_1_fun/sub | solution.py:39
  76.8 3.7 %fusion.59 = bf16[12,64,384]{2,1,0:T(8,128)(2,1)S(1)} fusion(bf16[384,12,64]{0,2,1:T(8,128)(2,1)S(1)} %bitcast.66, f32[12,384,384]{1,2,0:T(8,128)} %get-tuple-element.36, f32[12,384]{1,0:T(8,128)S(1)} %get-tuple-element.35), kind=kOutput, calls=%fused_computation.63 | convolution fusion | flops 230326272 | bytes 8275968 | tf_op jit(solution)/shard_map/cond/branch_1_fun/hqk,khc->qhc/dot_general | solution.py:41
  80.5 7.1 %fusion.42 = bf16[384,4096]{1,0:T(8,128)(2,1)} fusion(bf16[384,768]{0,1:T(8,128)(2,1)S(1)} %bitcast.76, bf16[4,4096,768]{2,1,0:T(8,128)(2,1)} %get-tuple-element.25), kind=kOutput, calls=%fused_computation.46 | convolution fusion | flops 2415919104 | bytes 10027008 | tf_op jit(solution)/shard_map/cond/branch_1_fun/dot_general | solution.py:46
  87.6 1.1 broadcast.57
  89.5 35.7 %all-reduce.2.cloned.1.call-done = bf16[128,4096]{1,0:T(8,128)(2,1)} async-done(((bf16[128,4096]{1,0:T(8,128)(2,1)}), bf16[128,4096]{1,0:T(8,128)(2,1)}) %all-reduce.2.cloned.1.call-update) | async-done | bytes 1048592 | tf_op jit(solution)/shard_map/psum | solution.py:91
  125.2 1.8 add_convert_fusion
  127.0 1.5 collective-permute-start.4
  128.5 37.6 %reduce-scatter.2.cloned.1.call-done = bf16[96,4096]{1,0:T(8,128)(2,1)} async-done(((bf16[384,4096]{1,0:T(8,128)(2,1)}), bf16[96,4096]{1,0:T(8,128)(2,1)}) %reduce-scatter.2.cloned.1.call-update) | async-done | bytes 786448 | tf_op jit(solution)/shard_map/reduce_scatter | solution.py:87
  166.1 1.3 add_convert_fusion.1
  167.5 1.5 collective-permute-start.3
  169.0 20.3 %collective-permute-done.3 = bf16[96,4096]{1,0:T(8,128)(2,1)S(1)} collective-permute-done((bf16[96,4096]{1,0:T(8,128)(2,1)S(1)}, bf16[96,4096]{1,0:T(8,128)(2,1)S(1)}, u32[]{:S(2)}, u32[]{:S(2)}) %collective-permute-start.3) | collective-permute-done | bytes 786464 | tf_op jit(solution)/shard_map/ppermute | solution.py:12
  189.3 0.9 copy.36
  190.2 1.0 copy.37
  (27 shorter events, 4.1 us)
Async XLA Ops:
  7.2 36.8 %copy-start = (bf16[96,4096]{1,0:T(8,128)(2,1)S(1)}, bf16[96,4096]{1,0:T(8,128)(2,1)}, u32[]{:S(2)}) copy-start(bf16[96,4096]{1,0:T(8,128)(2,1)} %param.7) | copy-start | bytes 2359300
  7.2 118.0 %all-reduce.2.cloned.1.call-start = ((), (), s32[]{:S(2)}) async-start(), calls=%async_computation.2 | async-start | bytes 2097152 | tf_op jit(solution)/shard_map/psum | solution.py:91
  7.2 12.3 %collective-permute-start = (bf16[96,4096]{1,0:T(8,128)(2,1)}, bf16[96,4096]{1,0:T(8,128)(2,1)S(1)}, u32[]{:S(2)}, u32[]{:S(2)}) collective-permute-start(bf16[96,4096]{1,0:T(8,128)(2,1)} %param.7), channel_id=1, source_target_pairs={{0,1},{1,2},{2,3},{3,0},{4,5},{5,6},{6,7},{7,4},{8,9},{9,10},{10,1... | collective-permute-start | bytes 2359304 | tf_op jit(solution)/shard_map/ppermute | solution.py:59
  19.6 11.4 %collective-permute-start.1 = (bf16[96,4096]{1,0:T(8,128)(2,1)S(1)}, bf16[96,4096]{1,0:T(8,128)(2,1)S(1)}, u32[]{:S(2)}, u32[]{:S(2)}) collective-permute-start(bf16[96,4096]{1,0:T(8,128)(2,1)S(1)} %collective-permute-done), channel_id=1, source_target_pairs={{0,1},{1,2},{2,3},{3,0},{4,5},{5,6},{6,7},{7,4},{8,9},{9,10},{10,1... | collective-permute-start | bytes 2359304 | tf_op jit(solution)/shard_map/ppermute | solution.py:59
  31.0 11.4 %collective-permute-start.2 = (bf16[96,4096]{1,0:T(8,128)(2,1)S(1)}, bf16[96,4096]{1,0:T(8,128)(2,1)S(1)}, u32[]{:S(2)}, u32[]{:S(2)}) collective-permute-start(bf16[96,4096]{1,0:T(8,128)(2,1)S(1)} %collective-permute-done.1), channel_id=1, source_target_pairs={{0,1},{1,2},{2,3},{3,0},{4,5},{5,6},{6,7},{7,4},{8,9},{9,10},{10,1... | collective-permute-start | bytes 2359304 | tf_op jit(solution)/shard_map/ppermute | solution.py:59
  43.8 1.2 copy-start.2
  43.8 1.2 copy-start.3
  88.7 77.4 %copy-start.1 = (bf16[96,4096]{1,0:T(8,128)(2,1)S(1)}, bf16[96,4096]{1,0:T(8,128)(2,1)}, u32[]{:S(2)}) copy-start(bf16[96,4096]{1,0:T(8,128)(2,1)} %param.7) | copy-start | bytes 2359300
  88.7 77.4 %reduce-scatter.2.cloned.1.call-start = ((), (), s32[]{:S(2)}) async-start(), calls=%async_computation.1 | async-start | bytes 3932160 | tf_op jit(solution)/shard_map/reduce_scatter | solution.py:87
  127.0 42.0 %collective-permute-start.4 = (bf16[128,4096]{1,0:T(8,128)(2,1)S(1)}, bf16[128,4096]{1,0:T(8,128)(2,1)S(1)}, u32[]{:S(2)}, u32[]{:S(2)}) collective-permute-start(bf16[128,4096]{1,0:T(8,128)(2,1)S(1)} %add_convert_fusion), channel_id=1, source_target_pairs={{0,4},{4,8},{8,12},{12,16},{16,20},{20,24},{24,28},{28,0},{1,5},{5... | collective-permute-start | bytes 3145736 | tf_op jit(solution)/shard_map/ppermute | solution.py:12
  167.5 21.9 %collective-permute-start.3 = (bf16[96,4096]{1,0:T(8,128)(2,1)S(1)}, bf16[96,4096]{1,0:T(8,128)(2,1)S(1)}, u32[]{:S(2)}, u32[]{:S(2)}) collective-permute-start(bf16[96,4096]{1,0:T(8,128)(2,1)S(1)} %add_convert_fusion.1), channel_id=1, source_target_pairs={{0,4},{4,8},{8,12},{12,16},{16,20},{20,24},{24,28},{28,0},{1,5},{5... | collective-permute-start | bytes 2359304 | tf_op jit(solution)/shard_map/ppermute | solution.py:12
Sparse Core Ops, SparseCore 0:
  88.8 36.3 all-reduce.1
  127.7 38.3 reduce-scatter.1
